TPU v7x, 16 devices: a 4x2x1 block of a 4x4x8 slice. The times are simulated.
16 devices in a mesh: data: 2 (over y, z), expert: 8 (over x, core).
Axes of the slice: x: 4, y: 2, z: 1, core: 2. Of those that a mesh axis runs over, the one named last changes fastest.
The devices are a block of a 4x4x8 slice.
Arguments:
- x_a: bfloat16 [2048, 2048], P(('data', 'expert')), parts along dimension 0
- idx_a: int32 [2048, 6], P(('data', 'expert')), parts along dimension 0
- gate_a: float32 [2048, 6], P(('data', 'expert')), parts along dimension 0
- x_b: bfloat16 [2048, 2048], P(('data', 'expert')), parts along dimension 0
- idx_b: int32 [2048, 6], P(('data', 'expert')), parts along dimension 0
- gate_b: float32 [2048, 6], P(('data', 'expert')), parts along dimension 0
- w_up: bfloat16 [64, 2048, 1408], P('expert')
- w_down: bfloat16 [64, 1408, 2048], P('expert')
Outputs:
- output 1: bfloat16 [2048, 2048], P(('data', 'expert')), parts along dimension 0
- output 2: bfloat16 [2048, 2048], P(('data', 'expert')), parts along dimension 0
There are 2 independent parts. A program takes and returns all parts, laid end to end along the dimension named above; an argument that names none is the same for every part.
All inputs are finite; a program needn't handle non-finite values.
Results may differ from a plain program's by a relative error of at most 0.00553068.
Values are sent between devices in bfloat16 or wider.
A program may use at most 768 MiB of HBM per device.

v0:
```python
import functools

import jax
import jax.numpy as jnp
from jax import lax
from jax.experimental import pallas as pl
from jax.experimental.pallas import tpu as pltpu
from jax.sharding import PartitionSpec as P

F32 = jnp.float32
BF16 = jnp.bfloat16
CW = 256
TW = 512


def moe_kernel(dims, idx_a, gate_a, idx_b, gate_b, xa_hbm, xb_hbm, wu_hbm, wd_hbm, ya_hbm, yb_hbm,
               xall, buf, hid, w1, w2, coef, pick, pick_f, meta, osum, part, dbuf, cbuf, rbuf, fbuf, ybuf,
               meta_send, meta_recv, x_sem, ag_send, ag_recv, fwd_send, core_send, core_recv,
               w1_sem, w2_sem, d_send, d_recv, r_send, r_recv, f_send, f_recv, y_sem):
    n_dev, n_chip, tok, k_top, d_model, d_ff, n_exp, load, cap = dims
    lanes = coef.shape[-1]
    rows = n_dev * load
    half = tok // 2
    pair = 2 * load
    n_col = d_model // CW
    n_step = 2 * n_col
    bounds = [(t, min(TW, d_ff - t)) for t in range(0, d_ff, TW)]
    n_tile = len(bounds)
    n_slot_p, n_slot_d, n_slot_f = part.shape[0], dbuf.shape[0], fbuf.shape[0]
    e_half = n_exp // 2
    n_slot_w2 = w2.shape[0]

    me = lax.axis_index('expert')
    chip, core = me // 2, lax.rem(me, 2)
    other = 1 - core
    right_c, left_c, far_c = lax.rem(chip + 1, n_chip), lax.rem(chip + n_chip - 1, n_chip), lax.rem(chip + 2, n_chip)
    partner = chip * 2 + other
    side = (right_c * 2 + core, left_c * 2 + core)

    def remote(src, dst, send, recv, dev):
        return pltpu.make_async_remote_copy(src_ref=src, dst_ref=dst, send_sem=send, recv_sem=recv,
                                            device_id={'expert': dev}, device_id_type=pl.DeviceIdType.MESH)

    def w1_copy(e, t):
        lo, width = bounds[t]
        return pltpu.make_async_copy(wu_hbm.at[e, :, pl.ds(lo, width)], w1.at[t, :, pl.ds(0, width)], w1_sem.at[t])

    def w2_copy(q):
        step, part_id = q // 2, lax.rem(q, 2)
        col = pl.multiple_of(lax.rem(step, n_col) * CW, CW)
        slot = lax.rem(q, n_slot_w2)
        return pltpu.make_async_copy(wd_hbm.at[pl.ds(part_id * e_half, e_half), :, pl.ds(col, CW)], w2.at[slot], w2_sem.at[slot])

    def block(m, c, r0=0, n=tok, k=None):
        k = core if k is None else k
        return xall.at[m, c, pl.ds(pl.multiple_of(k * tok + r0, 16), n), :]

    def own_load(m):
        return pltpu.make_async_copy((xa_hbm, xb_hbm)[m], block(m, chip), x_sem.at[m])

    def own_send(m, d, h):
        ref = block(m, chip, h * half, half)
        return remote(ref, ref, ag_send.at[m, d, h], ag_recv.at[m, d, h], side[d])

    def own_arrival(m, d, h):
        ref = block(m, (left_c, right_c)[d], h * half, half)
        return remote(ref, ref, ag_send.at[m, d, h], ag_recv.at[m, d, h], side[d])

    def forward(m, d):
        ref = block(m, (left_c, right_c)[d], d * half, half)
        return remote(ref, ref, fwd_send.at[m, d], ag_recv.at[m, d, 2], side[d])

    def far_arrival(m, d):
        ref = block(m, far_c, d * half, half)
        return remote(ref, ref, fwd_send.at[m, d], ag_recv.at[m, d, 2], side[d])

    def to_partner(m, i):
        ref = block(m, (chip, right_c, left_c, far_c)[i])
        return remote(ref, ref, core_send.at[m, i], core_recv.at[m, i], partner)

    def from_partner(m, i):
        ref = block(m, (chip, right_c, left_c, far_c)[i], k=other)
        return remote(ref, ref, core_send.at[m, i], core_recv.at[m, i], partner)

    def start_own(m):
        own_send(m, 0, 0).start()
        own_send(m, 1, 1).start()
        own_send(m, 0, 1).start()
        own_send(m, 1, 0).start()
        to_partner(m, 0).start()

    def relay_first(m):
        for d in range(2):
            own_arrival(m, d, d).wait_recv()
            forward(m, d).start()

    def relay_second(m):
        own_arrival(m, 1, 0).wait_recv()
        to_partner(m, 1).start()
        own_arrival(m, 0, 1).wait_recv()
        to_partner(m, 2).start()

    def relay_far(m):
        for d in range(2):
            far_arrival(m, d).wait_recv()
        to_partner(m, 3).start()

    def routing(m):
        lane = lax.broadcasted_iota(jnp.int32, (1, lanes), 1)
        lane_e = jnp.where(lane < n_exp * load, me * n_exp + lane // load, -1).astype(F32)
        lane_r = lax.rem(lane, load).astype(F32)
        row_id = lax.broadcasted_iota(jnp.int32, (tok, tok), 0)
        col_id = lax.broadcasted_iota(jnp.int32, (tok, tok), 1)
        below = jnp.where(col_id < row_id, 1.0, 0.0).astype(BF16)

        def one_source(s, before):
            facts = jnp.concatenate([meta[s], jnp.zeros((tok - meta.shape[1], tok), F32)], axis=0).T
            hit = jnp.zeros((tok, lanes), F32)
            gate = jnp.zeros((tok, lanes), F32)
            for j in range(k_top):
                same = facts[:, 16 * m + j:16 * m + j + 1] == lane_e
                hit = jnp.where(same, 1.0, hit)
                gate = jnp.where(same, facts[:, 16 * m + 8 + j:16 * m + 9 + j], gate)
            rank = jnp.dot(below, hit.astype(BF16), preferred_element_type=F32)
            keep = (hit > 0.0) & (rank == lane_r) & (before + rank < float(cap))
            gate = jnp.where(keep, gate, 0.0)
            hi = (gate * 0.9921875).astype(BF16)
            rest = gate - hi.astype(F32)
            mid = rest.astype(BF16)
            low = (rest - mid.astype(F32)).astype(BF16)
            coef[m, 0, s] = hi
            coef[m, 1, s] = mid
            coef[m, 2, s] = low
            chosen = jnp.where(keep, 1.0, 0.0).T
            return before + jnp.sum(hit, axis=0, keepdims=True), chosen

        before = jnp.zeros((1, lanes), F32)
        for c in range(n_chip):
            for k in range(2):
                before, chosen = one_source(2 * c + k, before)
                for e in range(n_exp):
                    pick_f[e * pair + k * load:e * pair + (k + 1) * load, k * tok:(k + 1) * tok] = chosen[e * load:(e + 1) * load]
            pick[m, c] = pick_f[...].astype(BF16)

    def gather(m, c):
        for n in range(0, d_model, 512):
            got = jnp.dot(pick[m, c], xall[m, c, :, n:n + 512], preferred_element_type=F32).astype(BF16)
            for e in range(n_exp):
                buf[e, pl.ds(pl.multiple_of(c * pair, 16), pair), n:n + 512] = got[e * pair:(e + 1) * pair]

    def up(m, e):
        for t, (lo, width) in enumerate(bounds):
            w1_copy(e, t).wait()
            acc = jnp.dot(buf[e], w1[t, :, 0:width], preferred_element_type=F32)
            hid[m, e, :, lo:lo + width] = jax.nn.gelu(acc, approximate=True).astype(BF16)
            nxt = m * n_exp + e + 1

            @pl.when(nxt < 2 * n_exp)
            def _():
                w1_copy(lax.rem(nxt, n_exp), t).start()

    def down(m, k):
        slot = lax.rem(k, n_slot_p)
        for p in range(2):
            q = 2 * k + p
            w2_copy(q).wait()
            for i in range(e_half):
                e = p * e_half + i
                out = jnp.dot(hid[m, e], w2[lax.rem(q, n_slot_w2), i], preferred_element_type=F32)
                for s in range(n_dev):
                    osum[s, e * load:(e + 1) * load, :] = out[s * load:(s + 1) * load]

            @pl.when(q + n_slot_w2 < 2 * n_step)
            def _():
                w2_copy(q + n_slot_w2).start()

        @pl.when(k >= n_slot_p)
        def _():
            core_part(k - n_slot_p).wait_send()
        for s in range(n_dev):
            rhs = osum[s].astype(BF16)
            acc = jnp.dot(coef[m, 0, s], rhs, preferred_element_type=F32)
            acc += jnp.dot(coef[m, 1, s], rhs, preferred_element_type=F32)
            acc += jnp.dot(coef[m, 2, s], rhs, preferred_element_type=F32)
            part[slot, s % 2, s // 2] = acc
        core_part(k).start()

    def core_part(k):
        ps, ds = lax.rem(k, n_slot_p), lax.rem(k, n_slot_d)
        return remote(part.at[ps, other], dbuf.at[ds], d_send.at[ps], d_recv.at[ds], partner)

    def far_part(k, d):
        s = lax.rem(k, n_slot_d)
        return remote(cbuf.at[s, far_c, pl.ds(d * half, half)], rbuf.at[s, d], r_send.at[s, d], r_recv.at[s, d], side[d])

    def near_part(k, d, h):
        s, f = lax.rem(k, n_slot_d), lax.rem(k, n_slot_f)
        return remote(cbuf.at[s, (right_c, left_c)[d], pl.ds(h * half, half)], fbuf.at[f, d, pl.ds(h * half, half)],
                      f_send.at[s, d, h], f_recv.at[f, d, h], side[d])

    def y_copy(k, hbm):
        s = lax.rem(k, n_slot_d)
        col = pl.multiple_of(lax.rem(k, n_col) * CW, CW)
        return pltpu.make_async_copy(ybuf.at[s], hbm.at[:, pl.ds(col, CW)], y_sem.at[s])

    def drain_sends(k):
        for d in range(2):
            far_part(k, d).wait_send()
            near_part(k, d, 0).wait_send()
            near_part(k, d, 1).wait_send()

    def stage2(k):
        @pl.when(k >= n_slot_d)
        def _():
            drain_sends(k - n_slot_d)
        core_part(k).wait_recv()
        s = lax.rem(k, n_slot_d)
        ps = lax.rem(k, n_slot_p)
        for c in range(n_chip):
            cbuf[s, c] = part[ps, core, c] + dbuf[s, c]
        for d in range(2):
            far_part(k, d).start()
            near_part(k, d, 1 - d).start()

    def stage3(k):
        s = lax.rem(k, n_slot_d)
        for d in range(2):
            far_part(k, d).wait_recv()
            c = (right_c, left_c)[d]
            cbuf[s, c, d * half:(d + 1) * half] = cbuf[s, c, d * half:(d + 1) * half] + rbuf[s, d]
            near_part(k, d, d).start()

    def stage4(k, m, hbm):
        s, f = lax.rem(k, n_slot_d), lax.rem(k, n_slot_f)

        @pl.when(k >= n_slot_d)
        def _():
            y_copy(k - n_slot_d, hbm).wait()
        for d in range(2):
            for h in range(2):
                near_part(k, d, h).wait_recv()
        col = pl.multiple_of(lax.rem(k, n_col) * CW, CW)
        x_own = xall[m, chip, pl.ds(pl.multiple_of(core * tok, 16), tok), pl.ds(col, CW)].astype(F32)
        ybuf[s] = (x_own + (cbuf[s, chip] + fbuf[f, 0] + fbuf[f, 1])).astype(BF16)
        y_copy(k, hbm).start()

    def finish(k):
        @pl.when((k >= 1) & (k < n_step + 1))
        def _():
            stage2(k - 1)

        @pl.when((k >= 2) & (k < n_step + 2))
        def _():
            stage3(k - 2)

        @pl.when((k >= 3) & (k < n_col + 3))
        def _():
            stage4(k - 3, 0, ya_hbm)

        @pl.when(k >= n_col + 3)
        def _():
            stage4(k - 3, 1, yb_hbm)

    own_load(0).start()
    own_load(1).start()
    for t in range(n_tile):
        w1_copy(0, t).start()
    for q in range(n_slot_w2):
        w2_copy(jnp.int32(q)).start()

    barrier = pltpu.get_barrier_semaphore()
    for i in range(1, n_dev):
        pl.semaphore_signal(barrier, inc=1, device_id={'expert': lax.rem(me + i, n_dev)}, device_id_type=pl.DeviceIdType.MESH)

    for i, (ref, as_f32) in enumerate(((idx_a, True), (gate_a, False), (idx_b, True), (gate_b, False))):
        meta[me, 8 * i:8 * i + k_top] = ref[...].astype(F32) if as_f32 else ref[...]
        meta[me, 8 * i + k_top:8 * i + 8] = jnp.zeros((8 - k_top, tok), F32)
    pick_f[...] = jnp.zeros_like(pick_f)
    for s in range(n_dev):
        osum[s, n_exp * load:lanes] = jnp.zeros((lanes - n_exp * load, CW), F32)

    own_load(0).wait()
    pl.semaphore_wait(barrier, n_dev - 1)

    def meta_copy(i):
        return remote(meta.at[me], meta.at[me], meta_send.at[i], meta_recv.at[i], lax.rem(me + i, n_dev))

    def meta_arrival(i):
        src = lax.rem(me + n_dev - i, n_dev)
        return remote(meta.at[src], meta.at[src], meta_send.at[i], meta_recv.at[i], lax.rem(me + i, n_dev))

    for i in range(1, n_dev):
        meta_copy(i).start()
    start_own(0)
    for i in range(1, n_dev):
        meta_arrival(i).wait_recv()
    routing(0)
    relay_first(0)
    own_load(1).wait()
    start_own(1)
    routing(1)
    relay_second(0)
    from_partner(0, 0).wait_recv()
    gather(0, chip)
    from_partner(0, 1).wait_recv()
    gather(0, right_c)
    from_partner(0, 2).wait_recv()
    gather(0, left_c)
    relay_far(0)
    from_partner(0, 3).wait_recv()
    gather(0, far_c)

    def up_a(e, carry):
        @pl.when(e == 2)
        def _():
            relay_first(1)

        @pl.when(e == 5)
        def _():
            relay_second(1)
        up(0, e)
        return carry

    lax.fori_loop(0, n_exp, up_a, 0)

    def first_steps(k, carry):
        down(0, k)

        @pl.when(k == 0)
        def _():
            relay_far(1)
            for i in range(4):
                from_partner(1, i).wait_recv()
            for c in range(n_chip):
                gather(1, c)
        finish(k)
        up(1, k)
        return carry

    lax.fori_loop(0, n_col, first_steps, 0)

    def last_steps(k, carry):
        down(1, k)
        finish(k)
        return carry

    lax.fori_loop(n_col, n_step, last_steps, 0)

    def drain(k, carry):
        finish(k)
        return carry

    lax.fori_loop(n_step, n_step + 3, drain, 0)

    for i in range(1, n_dev):
        meta_copy(i).wait_send()
    for m in range(2):
        for d in range(2):
            for h in range(2):
                own_send(m, d, h).wait_send()
            forward(m, d).wait_send()
        for i in range(4):
            to_partner(m, i).wait_send()
    for k in range(n_step - n_slot_p, n_step):
        core_part(jnp.int32(k)).wait_send()
    for k in range(n_step - n_slot_d, n_step):
        drain_sends(jnp.int32(k))
        y_copy(jnp.int32(k), yb_hbm).wait()


def solution(mesh):
    n_dev = mesh.shape['expert']
    row_spec = P(('data', 'expert'), None)
    weight_spec = P('expert', None, None)

    def device_fn(x_a, idx_a, gate_a, x_b, idx_b, gate_b, w_up, w_down):
        tok, d_model = x_a.shape
        k_top = idx_a.shape[1]
        n_exp, _, d_ff = w_up.shape
        n_chip = n_dev // 2
        cap = tok * k_top // n_exp
        load = 2 * tok * k_top // (n_exp * n_dev)
        lanes = -(-n_exp * load // 128) * 128
        rows = n_dev * load
        half = tok // 2
        dims = (n_dev, n_chip, tok, k_top, d_model, d_ff, n_exp, load, cap)
        dma = pltpu.SemaphoreType.DMA
        any_spec = pl.BlockSpec(memory_space=pl.ANY)
        vmem_spec = pl.BlockSpec(memory_space=pltpu.VMEM)
        n_tile = -(-d_ff // TW)
        scratch = [
            pltpu.VMEM((2, n_chip, 2 * tok, d_model), BF16),
            pltpu.VMEM((n_exp, rows, d_model), BF16),
            pltpu.VMEM((2, n_exp, rows, d_ff), BF16),
            pltpu.VMEM((n_tile, d_model, TW), BF16),
            pltpu.VMEM((3, n_exp // 2, d_ff, CW), BF16),
            pltpu.VMEM((2, 3, n_dev, tok, lanes), BF16),
            pltpu.VMEM((2, n_chip, 2 * n_exp * load, 2 * tok), BF16),
            pltpu.VMEM((2 * n_exp * load, 2 * tok), F32),
            pltpu.VMEM((n_dev, 32, tok), F32),
            pltpu.VMEM((n_dev, lanes, CW), F32),
            pltpu.VMEM((2, 2, n_chip, tok, CW), F32),
            pltpu.VMEM((4, n_chip, tok, CW), F32),
            pltpu.VMEM((4, n_chip, tok, CW), F32),
            pltpu.VMEM((4, 2, half, CW), F32),
            pltpu.VMEM((8, 2, tok, CW), F32),
            pltpu.VMEM((4, tok, CW), BF16),
            dma((n_dev,)), dma((n_dev,)), dma((2,)),
            dma((2, 2, 2)), dma((2, 2, 3)), dma((2, 2)),
            dma((2, 4)), dma((2, 4)),
            dma((n_tile,)), dma((3,)),
            dma((2,)), dma((4,)),
            dma((4, 2)), dma((4, 2)),
            dma((4, 2, 2)), dma((8, 2, 2)), dma((4,)),
        ]
        return pl.pallas_call(
            functools.partial(moe_kernel, dims),
            out_shape=(jax.ShapeDtypeStruct(x_a.shape, BF16), jax.ShapeDtypeStruct(x_b.shape, BF16)),
            in_specs=[vmem_spec] * 4 + [any_spec] * 4,
            out_specs=(any_spec, any_spec),
            scratch_shapes=scratch,
            compiler_params=pltpu.CompilerParams(collective_id=0, has_side_effects=True, vmem_limit_bytes=67043328),
        )(idx_a.T, gate_a.T, idx_b.T, gate_b.T, x_a, x_b, w_up, w_down)

    return jax.shard_map(device_fn, mesh=mesh, in_specs=(row_spec, row_spec, row_spec, row_spec, row_spec, row_spec, weight_spec, weight_spec), out_specs=(row_spec, row_spec), check_vma=False)
```

profile of v0, /device:TPU:112, one launch (start us, length us, event | category | flops | bytes accessed | tf_op | source)
XLA Modules:
  0.0 138.0 jit_solution(11109515450291260324)
XLA Ops:
  0.6 133.6 %shard_map.95 = (bf16[128,2048]{1,0:T(8,128)(2,1)}, bf16[128,2048]{1,0:T(8,128)(2,1)}) custom-call(s32[6,128]{1,0:T(8,128)} %bitcast.4, f32[6,128]{1,0:T(8,128)} %bitcast.5, s32[6,128]{1,0:T(8,128)} %bitcast.6, f32[6,128]{1,0:T(8,128)} %bitcast.7, bf16[128,2048]{1,0:T(8,128)(2,1)} %xa_hbm.1, bf16[128,2048]{1,0:T(8,128)(2,1)} %xb_hbm.1, ...), custom_call_target="tpu_custom_call" | custom-call | tf_op jit(solution)/shard_map/pallas_call | solution.py:416
  134.2 1.9 %copy.12 = bf16[128,2048]{1,0:T(8,128)(2,1)} copy(bf16[128,2048]{1,0:T(8,128)(2,1)} %get-tuple-element.4) | data formatting | bytes 1048576
  136.1 1.9 %copy.13 = bf16[128,2048]{1,0:T(8,128)(2,1)} copy(bf16[128,2048]{1,0:T(8,128)(2,1)} %get-tuple-element.5) | data formatting | bytes 1048576
where the time goes:
time: 138 us
  Pallas kernels  134 us (97%)
  local copies, waits for them, and re-layouts  3.76 us (3%)
    pallas_call x1, Pallas kernels, device_fn(): pl.pallas_call(functools.partial(moe_kernel, dims), out_shape=(jax.ShapeD...  134 us
    unnamed x2, local copies, waits for them, and re-layouts  3.76 us

commit v1 on v0

v1 whole, which is shorter than its diff:
```python
import functools

import jax
import jax.numpy as jnp
from jax import lax
from jax.experimental import pallas as pl
from jax.experimental.pallas import tpu as pltpu
from jax.sharding import PartitionSpec as P

F32 = jnp.float32
BF16 = jnp.bfloat16
CW = 256
TW = 512


def moe_kernel(dims, idx_a, gate_a, idx_b, gate_b, xa_hbm, xb_hbm, wu_hbm, wd_hbm, ya_ref, yb_ref,
               xall, buf, hid, w1, w2, coef, pick, pick_f, meta, osum, part, dbuf, cbuf, rbuf, fbuf,
               meta_send, meta_recv, x_sem, ag_send, ag_recv, fwd_send, core_send, core_recv,
               w1_sem, w2_sem, d_send, d_recv, r_send, r_recv, f_send, f_recv):
    n_dev, n_chip, tok, k_top, d_model, d_ff, n_exp, load, cap = dims
    lanes = coef.shape[-1]
    rows = n_dev * load
    half = tok // 2
    pair = 2 * load
    n_col = d_model // CW
    n_step = 2 * n_col
    bounds = [(t, min(TW, d_ff - t)) for t in range(0, d_ff, TW)]
    n_slot_p, n_slot_d, n_slot_c, n_slot_f = part.shape[0], dbuf.shape[0], cbuf.shape[0], fbuf.shape[0]
    n_slot_r = rbuf.shape[0]
    e_half = n_exp // 2
    n_slot_w1, n_slot_w2 = w1.shape[0], w2.shape[0]

    me = lax.axis_index('expert')
    chip, core = me // 2, lax.rem(me, 2)
    other = 1 - core
    right_c, left_c, far_c = lax.rem(chip + 1, n_chip), lax.rem(chip + n_chip - 1, n_chip), lax.rem(chip + 2, n_chip)
    partner = chip * 2 + other
    side = (right_c * 2 + core, left_c * 2 + core)

    def remote(src, dst, send, recv, dev):
        return pltpu.make_async_remote_copy(src_ref=src, dst_ref=dst, send_sem=send, recv_sem=recv,
                                            device_id={'expert': dev}, device_id_type=pl.DeviceIdType.MESH)

    def w1_copy(q):
        slot = lax.rem(q, n_slot_w1)
        return pltpu.make_async_copy(wu_hbm.at[lax.rem(q // 2, n_exp), pl.ds(lax.rem(q, 2) * (d_model // 2), d_model // 2)],
                                     w1.at[slot], w1_sem.at[slot])

    def w2_copy(q):
        step, part_id = q // 2, lax.rem(q, 2)
        col = pl.multiple_of(lax.rem(step, n_col) * CW, CW)
        slot = lax.rem(q, n_slot_w2)
        return pltpu.make_async_copy(wd_hbm.at[pl.ds(part_id * e_half, e_half), :, pl.ds(col, CW)], w2.at[slot], w2_sem.at[slot])

    def block(m, c, r0=0, n=tok, k=None):
        k = core if k is None else k
        return xall.at[m, c, pl.ds(pl.multiple_of(k * tok + r0, 16), n), :]

    def own_load(m):
        return pltpu.make_async_copy((xa_hbm, xb_hbm)[m], block(m, chip), x_sem.at[m])

    def own_send(m, d, h):
        ref = block(m, chip, h * half, half)
        return remote(ref, ref, ag_send.at[m, d, h], ag_recv.at[m, d, h], side[d])

    def own_arrival(m, d, h):
        ref = block(m, (left_c, right_c)[d], h * half, half)
        return remote(ref, ref, ag_send.at[m, d, h], ag_recv.at[m, d, h], side[d])

    def forward(m, d):
        ref = block(m, (left_c, right_c)[d], d * half, half)
        return remote(ref, ref, fwd_send.at[m, d], ag_recv.at[m, d, 2], side[d])

    def far_arrival(m, d):
        ref = block(m, far_c, d * half, half)
        return remote(ref, ref, fwd_send.at[m, d], ag_recv.at[m, d, 2], side[d])

    def to_partner(m, i):
        ref = block(m, (chip, right_c, left_c, far_c)[i])
        return remote(ref, ref, core_send.at[m, i], core_recv.at[m, i], partner)

    def from_partner(m, i):
        ref = block(m, (chip, right_c, left_c, far_c)[i], k=other)
        return remote(ref, ref, core_send.at[m, i], core_recv.at[m, i], partner)

    def relay_first(m):
        for d in range(2):
            own_arrival(m, d, d).wait_recv()
            forward(m, d).start()

    def relay_second(m):
        own_arrival(m, 1, 0).wait_recv()
        to_partner(m, 1).start()
        own_arrival(m, 0, 1).wait_recv()
        to_partner(m, 2).start()

    def relay_far(m):
        for d in range(2):
            far_arrival(m, d).wait_recv()
        to_partner(m, 3).start()

    def routing(m):
        lane = lax.broadcasted_iota(jnp.int32, (1, lanes), 1)
        lane_e = jnp.where(lane < n_exp * load, me * n_exp + lane // load, -1).astype(F32)
        lane_r = lax.rem(lane, load).astype(F32)
        row_id = lax.broadcasted_iota(jnp.int32, (tok, tok), 0)
        col_id = lax.broadcasted_iota(jnp.int32, (tok, tok), 1)
        below = jnp.where(col_id < row_id, 1.0, 0.0).astype(BF16)

        def one_source(s, before):
            facts = jnp.concatenate([meta[s], jnp.zeros((tok - meta.shape[1], tok), F32)], axis=0).T
            hit = jnp.zeros((tok, lanes), F32)
            gate = jnp.zeros((tok, lanes), F32)
            for j in range(k_top):
                same = facts[:, 16 * m + j:16 * m + j + 1] == lane_e
                hit = jnp.where(same, 1.0, hit)
                gate = jnp.where(same, facts[:, 16 * m + 8 + j:16 * m + 9 + j], gate)
            rank = jnp.dot(below, hit.astype(BF16), preferred_element_type=F32)
            keep = (hit > 0.0) & (rank == lane_r) & (before + rank < float(cap))
            gate = jnp.where(keep, gate, 0.0)
            hi = (gate * 0.9921875).astype(BF16)
            rest = gate - hi.astype(F32)
            mid = rest.astype(BF16)
            low = (rest - mid.astype(F32)).astype(BF16)
            coef[m, 0, s] = hi
            coef[m, 1, s] = mid
            coef[m, 2, s] = low
            chosen = jnp.where(keep, 1.0, 0.0).T
            return before + jnp.sum(hit, axis=0, keepdims=True), chosen

        before = jnp.zeros((1, lanes), F32)
        for c in range(n_chip):
            for k in range(2):
                before, chosen = one_source(2 * c + k, before)
                for e in range(n_exp):
                    pick_f[e * pair + k * load:e * pair + (k + 1) * load, k * tok:(k + 1) * tok] = chosen[e * load:(e + 1) * load]
            pick[m, c] = pick_f[...].astype(BF16)

    def gather(m, c):
        for n in range(0, d_model, 512):
            got = jnp.dot(pick[m, c], xall[m, c, :, n:n + 512], preferred_element_type=F32).astype(BF16)
            for e in range(n_exp):
                buf[e, pl.ds(pl.multiple_of(c * pair, 16), pair), n:n + 512] = got[e * pair:(e + 1) * pair]

    def up(m, e):
        q = 2 * (m * n_exp + e)
        depth = d_model // 2
        for h in range(2):
            w1_copy(q + h).wait()
        for lo, width in bounds:
            acc = jnp.dot(buf[e, :, 0:depth], w1[lax.rem(q, n_slot_w1), :, lo:lo + width], preferred_element_type=F32)
            acc += jnp.dot(buf[e, :, depth:], w1[lax.rem(q + 1, n_slot_w1), :, lo:lo + width], preferred_element_type=F32)
            hid[m, e, :, lo:lo + width] = jax.nn.gelu(acc, approximate=True).astype(BF16)
        for h in range(2):
            nxt = q + h + n_slot_w1

            @pl.when(nxt < 4 * n_exp)
            def _():
                w1_copy(nxt).start()

    def down(m, k):
        slot = lax.rem(k, n_slot_p)
        for p in range(2):
            w2_copy(2 * k + p).wait()

        @pl.when(k >= n_slot_p)
        def _():
            core_part(k - n_slot_p).wait_send()
        for e in range(n_exp):
            out = jnp.dot(hid[m, e], w2[lax.rem(2 * k + e // e_half, n_slot_w2), e % e_half], preferred_element_type=F32)
            for s in range(n_dev):
                osum[s, e * load:(e + 1) * load, :] = out[s * load:(s + 1) * load]
        for s in range(n_dev):
            rhs = osum[s].astype(BF16)
            acc = jnp.dot(coef[m, 0, s], rhs, preferred_element_type=F32)
            acc += jnp.dot(coef[m, 1, s], rhs, preferred_element_type=F32)
            acc += jnp.dot(coef[m, 2, s], rhs, preferred_element_type=F32)
            part[slot, s % 2, s // 2] = acc
        core_part(k).start()
        for p in range(2):
            q = 2 * k + p + n_slot_w2

            @pl.when(q < 2 * n_step)
            def _():
                w2_copy(q).start()

    def core_part(k):
        ps, ds = lax.rem(k, n_slot_p), lax.rem(k, n_slot_d)
        return remote(part.at[ps, other], dbuf.at[ds], d_send.at[ps], d_recv.at[ds], partner)

    def far_part(k, d):
        s, r = lax.rem(k, n_slot_c), lax.rem(k, n_slot_r)
        return remote(cbuf.at[s, far_c, pl.ds(d * half, half)], rbuf.at[r, d], r_send.at[s, d], r_recv.at[r, d], side[d])

    def near_part(k, d, h):
        s, f = lax.rem(k, n_slot_c), lax.rem(k, n_slot_f)
        return remote(cbuf.at[s, (right_c, left_c)[d], pl.ds(h * half, half)], fbuf.at[f, d, pl.ds(h * half, half)],
                      f_send.at[s, d, h], f_recv.at[f, d, h], side[d])

    def drain_sends(k):
        for d in range(2):
            far_part(k, d).wait_send()
            near_part(k, d, 0).wait_send()
            near_part(k, d, 1).wait_send()

    def stage2(k, late=False):
        @pl.when(k >= n_slot_c)
        def _():
            drain_sends(k - n_slot_c)
        core_part(k).wait_recv()
        s, ds, ps = lax.rem(k, n_slot_c), lax.rem(k, n_slot_d), lax.rem(k, n_slot_p)
        for c in range(n_chip):
            cbuf[s, c] = part[ps, core, c] + dbuf[ds, c]
        for d in range(2):
            far_part(k, d).start()
        if not late:
            near_halves(k)

    def near_halves(k):
        for d in range(2):
            near_part(k, d, 1 - d).start()

    def stage3(k):
        s = lax.rem(k, n_slot_c)
        for d in range(2):
            far_part(k, d).wait_recv()
            c = (right_c, left_c)[d]
            cbuf[s, c, d * half:(d + 1) * half] = cbuf[s, c, d * half:(d + 1) * half] + rbuf[lax.rem(k, n_slot_r), d]
            near_part(k, d, d).start()

    def stage4(k, m, y_ref):
        s, f = lax.rem(k, n_slot_c), lax.rem(k, n_slot_f)

        for d in range(2):
            for h in range(2):
                near_part(k, d, h).wait_recv()
        col = pl.multiple_of(lax.rem(k, n_col) * CW, CW)
        x_own = xall[m, chip, pl.ds(pl.multiple_of(core * tok, 16), tok), pl.ds(col, CW)].astype(F32)
        y_ref[:, pl.ds(col, CW)] = (x_own + (cbuf[s, chip] + fbuf[f, 0] + fbuf[f, 1])).astype(BF16)

    def stage4_at(k):
        @pl.when((k >= 0) & (k < n_col))
        def _():
            stage4(k, 0, ya_ref)

        @pl.when(k >= n_col)
        def _():
            stage4(k, 1, yb_ref)

    own_load(0).start()
    own_load(1).start()
    barrier = pltpu.get_barrier_semaphore()
    for i in range(1, n_dev):
        pl.semaphore_signal(barrier, inc=1, device_id={'expert': lax.rem(me + i, n_dev)}, device_id_type=pl.DeviceIdType.MESH)

    for i, (ref, as_f32) in enumerate(((idx_a, True), (gate_a, False), (idx_b, True), (gate_b, False))):
        meta[me, 8 * i:8 * i + k_top] = ref[...].astype(F32) if as_f32 else ref[...]
        meta[me, 8 * i + k_top:8 * i + 8] = jnp.zeros((8 - k_top, tok), F32)
    own_load(0).wait()
    own_load(1).wait()
    pl.semaphore_wait(barrier, n_dev - 1)

    def meta_copy(i):
        return remote(meta.at[me], meta.at[me], meta_send.at[i], meta_recv.at[i], lax.rem(me + i, n_dev))

    def meta_arrival(i):
        src = lax.rem(me + n_dev - i, n_dev)
        return remote(meta.at[src], meta.at[src], meta_send.at[i], meta_recv.at[i], lax.rem(me + i, n_dev))

    for i in range(1, n_dev):
        meta_copy(i).start()
    own_send(0, 0, 0).start()
    own_send(0, 1, 1).start()
    for q in range(n_slot_w1):
        w1_copy(jnp.int32(q)).start()
    for q in range(n_slot_w2):
        w2_copy(jnp.int32(q)).start()
    pick_f[...] = jnp.zeros_like(pick_f)
    for s in range(n_dev):
        osum[s, n_exp * load:lanes] = jnp.zeros((lanes - n_exp * load, CW), F32)
    to_partner(0, 0).start()
    for i in range(1, n_dev):
        meta_arrival(i).wait_recv()
    own_send(0, 0, 1).start()
    own_send(0, 1, 0).start()
    routing(0)
    relay_first(0)
    routing(1)
    relay_second(0)
    from_partner(0, 0).wait_recv()
    gather(0, chip)
    from_partner(0, 1).wait_recv()
    gather(0, right_c)
    from_partner(0, 2).wait_recv()
    gather(0, left_c)
    relay_far(0)
    own_send(1, 0, 0).start()
    own_send(1, 1, 1).start()
    to_partner(1, 0).start()
    from_partner(0, 3).wait_recv()
    gather(0, far_c)

    def up_a(e, carry):
        up(0, e)

        @pl.when(e == 0)
        def _():
            own_send(1, 0, 1).start()
            own_send(1, 1, 0).start()

        @pl.when(e == 3)
        def _():
            relay_first(1)

        @pl.when(e == 6)
        def _():
            relay_second(1)
        return carry

    lax.fori_loop(0, n_exp, up_a, 0)

    def first_steps(k, carry):
        down(0, k)

        @pl.when(k == 0)
        def _():
            for i, c in ((0, chip), (1, right_c)):
                from_partner(1, i).wait_recv()
                gather(1, c)
            stage2(k)
            relay_far(1)

        @pl.when(k == 1)
        def _():
            for i, c in ((2, left_c), (3, far_c)):
                from_partner(1, i).wait_recv()
                gather(1, c)

        @pl.when(k >= 2)
        def _():
            up(1, k - 2)
        stage4_at(k - 3)

        @pl.when(k >= 1)
        def _():
            stage2(k)
            stage3(k - 1)
        return carry

    lax.fori_loop(0, n_col, first_steps, 0)

    def rest_up(e, carry):
        up(1, e)
        return carry

    lax.fori_loop(n_col - 2, n_exp, rest_up, 0)

    def last_steps(k, carry):
        down(1, k)
        stage4_at(k - 3)
        stage2(k)
        stage3(k - 1)
        return carry

    lax.fori_loop(n_col, n_step - 1, last_steps, 0)
    last = jnp.int32(n_step - 1)
    down(1, last)
    stage4(last - 3, 1, yb_ref)
    stage2(last, late=True)
    stage3(last - 1)
    near_halves(last)
    stage4(last - 2, 1, yb_ref)
    stage3(last)
    stage4(last - 1, 1, yb_ref)
    stage4(last, 1, yb_ref)

    for i in range(1, n_dev):
        meta_copy(i).wait_send()
    for m in range(2):
        for d in range(2):
            for h in range(2):
                own_send(m, d, h).wait_send()
            forward(m, d).wait_send()
        for i in range(4):
            to_partner(m, i).wait_send()
    for k in range(n_step - n_slot_p, n_step):
        core_part(jnp.int32(k)).wait_send()
    for k in range(n_step - n_slot_c, n_step):
        drain_sends(jnp.int32(k))


def solution(mesh):
    n_dev = mesh.shape['expert']
    row_spec = P(('data', 'expert'), None)
    weight_spec = P('expert', None, None)

    def device_fn(x_a, idx_a, gate_a, x_b, idx_b, gate_b, w_up, w_down):
        tok, d_model = x_a.shape
        k_top = idx_a.shape[1]
        n_exp, _, d_ff = w_up.shape
        n_chip = n_dev // 2
        cap = tok * k_top // n_exp
        load = 2 * tok * k_top // (n_exp * n_dev)
        lanes = -(-n_exp * load // 128) * 128
        rows = n_dev * load
        half = tok // 2
        dims = (n_dev, n_chip, tok, k_top, d_model, d_ff, n_exp, load, cap)
        dma = pltpu.SemaphoreType.DMA
        any_spec = pl.BlockSpec(memory_space=pl.ANY)
        vmem_spec = pl.BlockSpec(memory_space=pltpu.VMEM)
        scratch = [
            pltpu.VMEM((2, n_chip, 2 * tok, d_model), BF16),
            pltpu.VMEM((n_exp, rows, d_model), BF16),
            pltpu.VMEM((2, n_exp, rows, d_ff), BF16),
            pltpu.VMEM((5, d_model // 2, d_ff), BF16),
            pltpu.VMEM((3, n_exp // 2, d_ff, CW), BF16),
            pltpu.VMEM((2, 3, n_dev, tok, lanes), BF16),
            pltpu.VMEM((2, n_chip, 2 * n_exp * load, 2 * tok), BF16),
            pltpu.VMEM((2 * n_exp * load, 2 * tok), F32),
            pltpu.VMEM((n_dev, 32, tok), F32),
            pltpu.VMEM((n_dev, lanes, CW), F32),
            pltpu.VMEM((2, 2, n_chip, tok, CW), F32),
            pltpu.VMEM((2, n_chip, tok, CW), F32),
            pltpu.VMEM((3, n_chip, tok, CW), F32),
            pltpu.VMEM((4, 2, half, CW), F32),
            pltpu.VMEM((5, 2, tok, CW), F32),
            dma((n_dev,)), dma((n_dev,)), dma((2,)),
            dma((2, 2, 2)), dma((2, 2, 3)), dma((2, 2)),
            dma((2, 4)), dma((2, 4)),
            dma((5,)), dma((3,)),
            dma((2,)), dma((2,)),
            dma((3, 2)), dma((4, 2)),
            dma((3, 2, 2)), dma((5, 2, 2)),
        ]
        return pl.pallas_call(
            functools.partial(moe_kernel, dims),
            out_shape=(pltpu.VMEM(x_a.shape, BF16), pltpu.VMEM(x_b.shape, BF16)),
            in_specs=[vmem_spec] * 4 + [any_spec] * 4,
            out_specs=(vmem_spec, vmem_spec),
            scratch_shapes=scratch,
            compiler_params=pltpu.CompilerParams(collective_id=0, has_side_effects=True, vmem_limit_bytes=65994752),
        )(idx_a.T, gate_a.T, idx_b.T, gate_b.T, x_a, x_b, w_up, w_down)

    return jax.shard_map(device_fn, mesh=mesh, in_specs=(row_spec, row_spec, row_spec, row_spec, row_spec, row_spec, weight_spec, weight_spec), out_specs=(row_spec, row_spec), check_vma=False)
```

time: 138 us -> 124 us (0.90)
  Pallas kernels: 134 us -> 121 us
  local copies, waits for them, and re-layouts: 3.76 us -> 1.59 us
    pallas_call x1, Pallas kernels: 134 us -> 121 us  [device_fn(): pl.pallas_call(functools.partial(moe_kernel, dims), out_shape=(pltpu.VMEM...]
    unnamed x2, local copies, waits for them, and re-layouts: 3.76 us -> 1.59 us
where the time goes in v1:
time: 124 us; the launch traced here: 123 us
  Pallas kernels  121 us (98%)
  local copies, waits for them, and re-layouts  1.59 us (1%)
    pallas_call x1, Pallas kernels, device_fn(): pl.pallas_call(functools.partial(moe_kernel, dims), out_shape=(pltpu.VMEM...  121 us

profile of v1, /device:TPU:112, one launch (start us, length us, event | category | flops | bytes accessed | tf_op | source)
XLA Modules:
  0.0 123.2 jit_solution(15322386776489458111)
XLA Ops:
  0.6 121.0 %shard_map.95 = (bf16[128,2048]{1,0:T(8,128)(2,1)S(1)}, bf16[128,2048]{1,0:T(8,128)(2,1)S(1)}) custom-call(s32[6,128]{1,0:T(8,128)} %bitcast.4, f32[6,128]{1,0:T(8,128)} %bitcast.5, s32[6,128]{1,0:T(8,128)} %bitcast.6, f32[6,128]{1,0:T(8,128)} %bitcast.7, bf16[128,2048]{1,0:T(8,128)(2,1)} %xa_hbm.1, bf16[128,2048]{1,0:T(8,128)(2,1)} %xb_hbm.1, ...), custom_call_target="tpu_custom_call" | custom-call | tf_op jit(solution)/shard_map/pallas_call | solution.py:435
  121.6 0.8 copy.12
  122.4 0.8 copy.13
